TPU v7x, 32 devices: a whole 2x2x4 slice. The times are simulated.
32 devices in a mesh: tp: 4 (over y, x), dp: 8 (over z, core).
Axes of the slice: x: 2, y: 2, z: 4, core: 2. Of those that a mesh axis runs over, the one named last changes fastest.
Arguments:
- activations: bfloat16 [2, 8192, 8192], P(None, 'dp', 'tp'), may hold values from -72 to 72
- out_grads: bfloat16 [2, 8192, 2048], P(None, 'dp'), may hold values from -2 to 2
- master: float32 [8192, 2, 2048], P(('tp', 'dp')), may hold values from -1.2 to 1.2
- first_moment: float32 [8192, 2, 2048], P(('tp', 'dp')), may hold values from -1.8 to 1.8
- second_moment: float32 [8192, 2, 2048], P(('tp', 'dp')), may hold values from 0.01 to 1
Outputs:
- new_master: float32 [8192, 2, 2048], P(('tp', 'dp'))
- new_first: float32 [8192, 2, 2048], P(('tp', 'dp'))
- new_second: float32 [8192, 2, 2048], P(('tp', 'dp'))
- weights: bfloat16 [8192, 2, 2048], P('tp')
All inputs are finite; a program needn't handle non-finite values.
Results may differ from a plain program's by a relative error of at most 0.0004.
Values may be sent and summed in bfloat16 or wider, within the bound.
A program may use at most 192 MiB of HBM per device.

v0:
```python
import math
import jax
import jax.numpy as jnp
from jax import lax
from jax.sharding import PartitionSpec as P

beta_first = 0.9
beta_second = 0.95
first_fix = 1.0 - 0.9**10
second_fix = 1.0 - 0.95**10
learn_rate = 0.01
decay_rate = 0.1
epsilon = 1e-08
limit_scale = 2.0


def reduce_rows(layer_acts, layer_grads):
    grad_own = lax.psum_scatter(
        jnp.einsum("ltr,ltc->rlc", layer_acts, layer_grads, preferred_element_type=jnp.float32),
        "dp",
        scatter_dimension=0,
        tiled=True,
    )
    partial_value = jnp.sum(grad_own * grad_own)
    return (grad_own, partial_value)


def adam_update(grad_own, master, first_moment, second_moment, clip_factor):
    clipped = clip_factor * grad_own
    new_first = beta_first * first_moment + (1.0 - beta_first) * clipped
    new_second = beta_second * second_moment + (1.0 - beta_second) * clipped * clipped
    step_dir = new_first / first_fix / (jnp.sqrt(new_second / second_fix) + epsilon)
    new_master = master - learn_rate * (step_dir + decay_rate * master)
    return (new_master, new_first, new_second)


def on_device(activations, out_grads, master, first_moment, second_moment):
    own_rows = master.shape[0]
    grad_own, layer_sum = reduce_rows(activations, out_grads)
    sum_squares = lax.psum(layer_sum, ("tp", "dp"))
    entries = (
        own_rows * lax.axis_size("tp") * lax.axis_size("dp") * master.shape[1] * master.shape[2]
    )
    limit = limit_scale * math.sqrt(entries)
    clip_factor = limit / jnp.maximum(jnp.sqrt(sum_squares), limit)
    new_master, new_first, new_second = adam_update(
        grad_own, master, first_moment, second_moment, clip_factor
    )
    rounded = new_master.astype(jnp.bfloat16)
    tp_rows = lax.all_gather(rounded, "dp", axis=0, tiled=True)
    return (new_master, new_first, new_second, tp_rows)


def solution(mesh):
    return jax.shard_map(
        on_device,
        mesh=mesh,
        in_specs=(
            P(None, "dp", "tp"),
            P(None, "dp", None),
            P(("tp", "dp"), None, None),
            P(("tp", "dp"), None, None),
            P(("tp", "dp"), None, None),
        ),
        out_specs=(
            P(("tp", "dp"), None, None),
            P(("tp", "dp"), None, None),
            P(("tp", "dp"), None, None),
            P("tp", None, None),
        ),
        check_vma=False,
    )
```

profile of v0, /device:TPU:0, one launch (start us, length us, event | category | flops | bytes accessed | tf_op | source)
XLA Modules:
  0.0 623.6 jit_solution(12652880110053405186)
XLA Ops:
  7.2 0.0 reduce-scatter.2.cloned.1.call-start
  7.2 25.6 %convolution_bitcast_fusion = f32[2048,2,2048]{0,2,1:T(8,128)} fusion(bf16[2,1024,2048]{2,1,0:T(8,128)(2,1)} %param.6, bf16[2,1024,2048]{2,1,0:T(8,128)(2,1)} %param.5), kind=kOutput, calls=%fused_computation | convolution fusion | flops 17179869184 | bytes 50331648 | tf_op jit(solution)/shard_map/ltr,ltc->rlc/dot_general | solution.py:19
  32.9 0.0 reduce-scatter.2.cloned.1.call-update
  32.9 0.0 all-gather.2.cloned.1.call-start
  32.9 7.2 %copy.13 = f32[256,2,2048]{0,2,1:T(8,128)} copy(f32[256,2,2048]{2,1,0:T(2,128)} %param.7) | data formatting | bytes 8388608 | tf_op args[2]
  40.1 7.2 %copy.9 = f32[256,2,2048]{0,2,1:T(8,128)} copy(f32[256,2,2048]{2,1,0:T(2,128)} %param.8) | data formatting | bytes 8388608 | tf_op args[3]
  47.4 313.8 %reduce-scatter.2.cloned.1.call-done = f32[256,2,2048]{0,2,1:T(8,128)} async-done(((f32[2048,2,2048]{0,2,1:T(8,128)}), f32[256,2,2048]{0,2,1:T(8,128)}) %reduce-scatter.2.cloned.1.call-update) | async-done | bytes 4194320 | tf_op jit(solution)/shard_map/reduce_scatter | solution.py:18
  361.2 3.9 multiply_reduce_fusion
  365.1 7.2 %copy.11 = f32[256,2,2048]{0,2,1:T(8,128)} copy(f32[256,2,2048]{2,1,0:T(2,128)} %param.9) | data formatting | bytes 8388608 | tf_op args[4]
  372.3 37.9 %psum.7 = f32[]{:T(128)} all-reduce(f32[]{:T(128)} %multiply_reduce_fusion), channel_id=1, replica_groups=mesh['tp'=4,'dp'=8] {'tp','dp'}, use_global_device_ids=true, to_apply=%region_2.0 | all-reduce | flops 1 | bytes 8 | tf_op jit(solution)/shard_map/psum | solution.py:40
  411.0 11.7 %fusion.1 = (bf16[256,2,2048]{0,2,1:T(8,128)(2,1)}, f32[256,2,2048]{0,2,1:T(8,128)}, f32[256,2,2048]{0,2,1:T(8,128)}, f32[256,2,2048]{0,2,1:T(8,128)}) fusion(f32[256,2,2048]{0,2,1:T(8,128)} %copy.13, f32[256,2,2048]{0,2,1:T(8,128)} %reduce-scatter.2.cloned.1.call-done, f32[]{:T(128)S(6)} %div.18, f32[256,2,2048]{0,2,1:T(8,128)} %copy.9, f32[256,2,2048]{0,2,1:T(8,128)} %copy.11), kind=kLoop, calls=%fused_computation.6 | loop fusion | flops 17825792 | bytes 31457284 | tf_op jit(solution)/shard_map/convert_element_type | solution.py:49
  422.7 0.0 all-gather.2.cloned.1.call-update
  422.7 7.3 %copy.14 = f32[256,2,2048]{2,1,0:T(2,128)} copy(f32[256,2,2048]{0,2,1:T(8,128)} %get-tuple-element.9) | data formatting | bytes 8388608
  430.0 7.7 %copy.15 = f32[256,2,2048]{2,1,0:T(2,128)} copy(f32[256,2,2048]{0,2,1:T(8,128)} %get-tuple-element.10) | data formatting | bytes 8388608
  437.7 7.3 %copy.16 = f32[256,2,2048]{2,1,0:T(2,128)} copy(f32[256,2,2048]{0,2,1:T(8,128)} %get-tuple-element.11) | data formatting | bytes 8388608
  445.0 130.3 %all-gather.2.cloned.1.call-done = bf16[2048,2,2048]{0,2,1:T(8,128)(2,1)} async-done(((bf16[256,2,2048]{0,2,1:T(8,128)(2,1)}), bf16[2048,2,2048]{0,2,1:T(8,128)(2,1)}) %all-gather.2.cloned.1.call-update) | async-done | bytes 16777232 | tf_op jit(solution)/shard_map/all_gather | solution.py:50
  575.3 41.5 %copy.17 = bf16[2048,2,2048]{2,1,0:T(2,128)(2,1)} copy(bf16[2048,2,2048]{0,2,1:T(8,128)(2,1)} %all-gather.2.cloned.1.call-done) | data formatting | bytes 33554432
Async XLA Ops:
  7.2 354.1 %reduce-scatter.2.cloned.1.call-start = ((), (), s32[]{:S(2)}) async-start(), calls=%async_computation.1 | async-start | bytes 37748736 | tf_op jit(solution)/shard_map/reduce_scatter | solution.py:18
  32.9 542.4 %all-gather.2.cloned.1.call-start = ((), (), s32[]{:S(2)}) async-start(), calls=%async_computation.2 | async-start | bytes 18874368 | tf_op jit(solution)/shard_map/all_gather | solution.py:50
Sparse Core Ops, SparseCore 0:
  33.0 328.1 reduce-scatter.1
  422.8 152.4 all-gather.1
where the time goes:
time: 626 us; the launch traced here: 624 us
  waiting for transfers between devices  444 us (71%)
  local copies, waits for them, and re-layouts  85.4 us (14%)
  blocking collectives  37.9 us (6%)
  matrix products  25.6 us (4%)
  other arithmetic  15.6 us (2%)
  between operations  14.8 us (2%)
    reduce_scatter x1, waiting for transfers between devices, reduce_rows(): lax.psum_scatter(jnp.einsum('ltr,ltc->rlc', layer_acts, layer_grads, pref...  314 us
    all_gather x1, waiting for transfers between devices, on_device(): tp_rows = lax.all_gather(rounded, 'dp', axis=0, tiled=True)  130 us
    unnamed x7, local copies, waits for them, and re-layouts  85.4 us
    psum x1, blocking collectives, on_device(): sum_squares = lax.psum(layer_sum, ('tp', 'dp'))  37.9 us
    dot_general x1, matrix products, reduce_rows(): jnp.einsum('ltr,ltc->rlc', layer_acts, layer_grads, preferred_element_typ...  25.6 us
  transfers between devices with their start and end apart: 2, of which 2 were waited for; matrix products, arithmetic and copies ran while one was open for 6% of the time, Pallas kernels for 0%

commit v1 on v0

--- a/solution.py
+++ b/solution.py
@@ -12,6 +12,19 @@
 decay_rate = 0.1
 epsilon = 1e-08
 limit_scale = 2.0
+
+
+def apply_patch(view, row_axis):
+    size_here = lax.axis_size(row_axis)
+    new = sorted(((b, (b + 1) % size_here) for b in range(size_here)))
+    part_now = view
+    panels = [part_now]
+    for it in tuple(range(1, size_here)):
+        part_now = lax.ppermute(part_now, axis_name=row_axis, perm=new)
+        panels.insert(0, part_now)
+    a_next = jnp.concatenate(panels, 0)
+    y2 = lax.axis_index(row_axis) + 1
+    return jnp.roll(a_next, y2 * view.shape[0], 0)
 
 
 def reduce_rows(layer_acts, layer_grads):
@@ -47,7 +60,7 @@
         grad_own, master, first_moment, second_moment, clip_factor
     )
     rounded = new_master.astype(jnp.bfloat16)
-    tp_rows = lax.all_gather(rounded, "dp", axis=0, tiled=True)
+    tp_rows = apply_patch(rounded, "dp")
     return (new_master, new_first, new_second, tp_rows)
 
 

time: 626 us -> 693 us (1.11)
  waiting for transfers between devices: 444 us -> 483 us
  local copies, waits for them, and re-layouts: 85.4 us -> 114 us
    ppermute x0 -> x7, waiting for transfers between devices: none -> 169 us  [apply_patch(): part_now = lax.ppermute(part_now, axis_name=row_axis, perm=new)]
    all_gather x1 -> x0, waiting for transfers between devices: 130 us -> none  [on_device(): tp_rows = lax.all_gather(rounded, 'dp', axis=0, tiled=True)]
    unnamed x7 -> x42, local copies, waits for them, and re-layouts: 85.4 us -> 106 us
    dynamic_slice x0 -> x1, local copies, waits for them, and re-layouts: none -> 6.96 us  [apply_patch(): return jnp.roll(a_next, y2 * view.shape[0], 0)]
  transfers between devices with their start and end apart: 2 -> 8, of which waited for: 2 -> 8; matrix products, arithmetic and copies ran while one was open for 6% -> 5% of each run, Pallas kernels for 0% -> 0%
where the time goes in v1:
time: 693 us; the launch traced here: 691 us
  waiting for transfers between devices  483 us (70%)
  local copies, waits for them, and re-layouts  114 us (16%)
  blocking collectives  37.9 us (5%)
  matrix products  25.6 us (4%)
  other arithmetic  15.2 us (2%)
  between operations  14.9 us (2%)
    reduce_scatter x1, waiting for transfers between devices, reduce_rows(): lax.psum_scatter(jnp.einsum('ltr,ltc->rlc', layer_acts, layer_grads, pref...  314 us
    ppermute x7, waiting for transfers between devices, apply_patch(): part_now = lax.ppermute(part_now, axis_name=row_axis, perm=new)  169 us
    unnamed x42, local copies, waits for them, and re-layouts  106 us
    psum x1, blocking collectives, on_device(): sum_squares = lax.psum(layer_sum, ('tp', 'dp'))  37.9 us
    dot_general x1, matrix products, reduce_rows(): jnp.einsum('ltr,ltc->rlc', layer_acts, layer_grads, preferred_element_typ...  25.6 us
  transfers between devices with their start and end apart: 8, of which 8 were waited for; matrix products, arithmetic and copies ran while one was open for 5% of the time, Pallas kernels for 0%

profile of v1, /device:TPU:0, one launch (start us, length us, event | category | flops | bytes accessed | tf_op | source)
XLA Modules:
  0.0 690.6 jit_solution(8069284192825838019)
XLA Ops:
  7.2 0.0 reduce-scatter.2.cloned.1.call-start
  7.2 25.6 %convolution_bitcast_fusion = f32[2048,2,2048]{0,2,1:T(8,128)} fusion(bf16[2,1024,2048]{2,1,0:T(8,128)(2,1)} %param.6, bf16[2,1024,2048]{2,1,0:T(8,128)(2,1)} %param.5), kind=kOutput, calls=%fused_computation | convolution fusion | flops 17179869184 | bytes 50331648 | tf_op jit(solution)/shard_map/ltr,ltc->rlc/dot_general | solution.py:32
  32.9 0.0 reduce-scatter.2.cloned.1.call-update
  32.9 7.2 %copy.13 = f32[256,2,2048]{0,2,1:T(8,128)} copy(f32[256,2,2048]{2,1,0:T(2,128)} %param.7) | data formatting | bytes 8388608 | tf_op args[2]
  40.1 7.2 %copy.9 = f32[256,2,2048]{0,2,1:T(8,128)} copy(f32[256,2,2048]{2,1,0:T(2,128)} %param.8) | data formatting | bytes 8388608 | tf_op args[3]
  47.3 313.9 %reduce-scatter.2.cloned.1.call-done = f32[256,2,2048]{0,2,1:T(8,128)} async-done(((f32[2048,2,2048]{0,2,1:T(8,128)}), f32[256,2,2048]{0,2,1:T(8,128)}) %reduce-scatter.2.cloned.1.call-update) | async-done | bytes 4194320 | tf_op jit(solution)/shard_map/reduce_scatter | solution.py:31
  361.2 3.9 multiply_reduce_fusion
  365.1 7.2 %copy.11 = f32[256,2,2048]{0,2,1:T(8,128)} copy(f32[256,2,2048]{2,1,0:T(2,128)} %param.9) | data formatting | bytes 8388608 | tf_op args[4]
  372.3 37.9 %psum.7 = f32[]{:T(128)} all-reduce(f32[]{:T(128)} %multiply_reduce_fusion), channel_id=1, replica_groups=mesh['tp'=4,'dp'=8] {'tp','dp'}, use_global_device_ids=true, to_apply=%region_2.0 | all-reduce | flops 1 | bytes 8 | tf_op jit(solution)/shard_map/psum | solution.py:53
  411.0 11.3 %fusion.1 = (bf16[256,2,2048]{0,2,1:T(8,128)(2,1)S(1)}, f32[256,2,2048]{0,2,1:T(8,128)}, f32[256,2,2048]{0,2,1:T(8,128)}, f32[256,2,2048]{0,2,1:T(8,128)}) fusion(f32[256,2,2048]{0,2,1:T(8,128)} %copy.13, f32[256,2,2048]{0,2,1:T(8,128)} %reduce-scatter.2.cloned.1.call-done, f32[]{:T(128)S(6)} %div.18, f32[256,2,2048]{0,2,1:T(8,128)} %copy.9, ...), kind=kLoop, calls=%fused_computation.23 | loop fusion | flops 17825792 | bytes 31457284 | tf_op jit(solution)/shard_map/convert_element_type | solution.py:62
  422.3 0.0 collective-permute-start
  422.3 27.3 %collective-permute-done = bf16[256,2,2048]{0,2,1:T(8,128)(2,1)S(1)} collective-permute-done((bf16[256,2,2048]{0,2,1:T(8,128)(2,1)S(1)}, bf16[256,2,2048]{0,2,1:T(8,128)(2,1)S(1)}, u32[]{:S(2)}, u32[]{:S(2)}) %collective-permute-start) | collective-permute-done | bytes 2097184 | tf_op jit(solution)/shard_map/ppermute | solution.py:23
  449.6 1.3 copy-done
  450.9 27.3 %collective-permute-done.1 = bf16[256,2,2048]{0,2,1:T(8,128)(2,1)S(1)} collective-permute-done((bf16[256,2,2048]{0,2,1:T(8,128)(2,1)S(1)}, bf16[256,2,2048]{0,2,1:T(8,128)(2,1)S(1)}, u32[]{:S(2)}, u32[]{:S(2)}) %collective-permute-start.1) | collective-permute-done | bytes 2097184 | tf_op jit(solution)/shard_map/ppermute | solution.py:23
  478.2 1.4 copy-done.2
  479.5 27.3 %collective-permute-done.2 = bf16[256,2,2048]{0,2,1:T(8,128)(2,1)S(1)} collective-permute-done((bf16[256,2,2048]{0,2,1:T(8,128)(2,1)S(1)}, bf16[256,2,2048]{0,2,1:T(8,128)(2,1)S(1)}, u32[]{:S(2)}, u32[]{:S(2)}) %collective-permute-start.2) | collective-permute-done | bytes 2097184 | tf_op jit(solution)/shard_map/ppermute | solution.py:23
  506.8 1.3 copy-done.4
  508.1 27.3 %collective-permute-done.3 = bf16[256,2,2048]{0,2,1:T(8,128)(2,1)S(1)} collective-permute-done((bf16[256,2,2048]{0,2,1:T(8,128)(2,1)S(1)}, bf16[256,2,2048]{0,2,1:T(8,128)(2,1)S(1)}, u32[]{:S(2)}, u32[]{:S(2)}) %collective-permute-start.3) | collective-permute-done | bytes 2097184 | tf_op jit(solution)/shard_map/ppermute | solution.py:23
  535.4 1.3 copy-done.6
  536.7 27.3 %collective-permute-done.4 = bf16[256,2,2048]{0,2,1:T(8,128)(2,1)S(1)} collective-permute-done((bf16[256,2,2048]{0,2,1:T(8,128)(2,1)S(1)}, bf16[256,2,2048]{0,2,1:T(8,128)(2,1)S(1)}, u32[]{:S(2)}, u32[]{:S(2)}) %collective-permute-start.4) | collective-permute-done | bytes 2097184 | tf_op jit(solution)/shard_map/ppermute | solution.py:23
  563.9 1.3 copy-done.8
  565.3 27.4 %collective-permute-done.5 = bf16[256,2,2048]{0,2,1:T(8,128)(2,1)} collective-permute-done((bf16[256,2,2048]{0,2,1:T(8,128)(2,1)S(1)}, bf16[256,2,2048]{0,2,1:T(8,128)(2,1)}, u32[]{:S(2)}, u32[]{:S(2)}) %collective-permute-start.5) | collective-permute-done | bytes 2097184 | tf_op jit(solution)/shard_map/ppermute | solution.py:23
  592.6 0.0 collective-permute-start.6
  592.6 7.3 %copy.14 = f32[256,2,2048]{2,1,0:T(2,128)} copy(f32[256,2,2048]{0,2,1:T(8,128)} %get-tuple-element.9) | data formatting | bytes 8388608
  599.9 7.3 %copy.15 = f32[256,2,2048]{2,1,0:T(2,128)} copy(f32[256,2,2048]{0,2,1:T(8,128)} %get-tuple-element.10) | data formatting | bytes 8388608
  607.2 7.3 %copy.16 = f32[256,2,2048]{2,1,0:T(2,128)} copy(f32[256,2,2048]{0,2,1:T(8,128)} %get-tuple-element.11) | data formatting | bytes 8388608
  614.5 5.7 collective-permute-done.6
  620.2 1.9 constant_dynamic-update-slice_fusion.15
  622.1 2.0 constant_dynamic-update-slice_fusion.14
  624.2 0.3 constant_dynamic-update-slice_fusion.13
  624.5 0.3 constant_dynamic-update-slice_fusion.12
  624.8 1.0 copy-done.5
  625.8 0.3 constant_dynamic-update-slice_fusion.11
  626.1 0.4 copy-done.3
  626.4 0.3 constant_dynamic-update-slice_fusion.10
  626.7 0.8 copy-done.1
  627.5 0.3 constant_dynamic-update-slice_fusion.9
  627.8 0.3 constant_dynamic-update-slice_fusion.8
  628.1 1.9 constant_dynamic-update-slice_fusion.7
  630.0 1.9 constant_dynamic-update-slice_fusion.6
  631.9 1.9 constant_dynamic-update-slice_fusion.5
  633.8 0.3 constant_dynamic-update-slice_fusion.4
  634.1 0.3 constant_dynamic-update-slice_fusion.3
  634.4 0.3 constant_dynamic-update-slice_fusion.2
  634.7 0.3 constant_dynamic-update-slice_fusion.1
  635.0 0.3 constant_dynamic-update-slice_fusion
  635.3 7.0 %constant_dynamic-slice_fusion = bf16[2048,2,2048]{0,2,1:T(8,128)(2,1)} fusion(bf16[4096,2,2048]{0,2,1:T(8,128)(2,1)S(1)} %constant_dynamic-update-slice_fusion, s32[]{:T(128)S(6)} %select_n.14), kind=kLoop, calls=%fused_computation.22 | loop fusion | bytes 33554436 | tf_op jit(solution)/shard_map/jit(_roll_dynamic)/dynamic_slice | solution.py:27
  642.3 41.5 %copy.17 = bf16[2048,2,2048]{2,1,0:T(2,128)(2,1)} copy(bf16[2048,2,2048]{0,2,1:T(8,128)(2,1)} %constant_dynamic-slice_fusion) | data formatting | bytes 33554432
  (17 shorter events, 0.0 us)
Async XLA Ops:
  7.2 354.1 %reduce-scatter.2.cloned.1.call-start = ((), (), s32[]{:S(2)}) async-start(), calls=%async_computation.1 | async-start | bytes 37748736 | tf_op jit(solution)/shard_map/reduce_scatter | solution.py:31
  422.3 27.3 %collective-permute-start = (bf16[256,2,2048]{0,2,1:T(8,128)(2,1)S(1)}, bf16[256,2,2048]{0,2,1:T(8,128)(2,1)S(1)}, u32[]{:S(2)}, u32[]{:S(2)}) collective-permute-start(bf16[256,2,2048]{0,2,1:T(8,128)(2,1)S(1)} %get-tuple-element.8), channel_id=1, source_target_pairs={{0,1},{1,2},{2,3},{3,4},{4,5},{5,6},{6,7},{7,0},{8,9},{9,10},{10,1... | collective-permute-start | bytes 6291464 | tf_op jit(solution)/shard_map/ppermute | solution.py:23
  449.6 1.3 copy-start
  450.9 27.3 %collective-permute-start.1 = (bf16[256,2,2048]{0,2,1:T(8,128)(2,1)S(1)}, bf16[256,2,2048]{0,2,1:T(8,128)(2,1)S(1)}, u32[]{:S(2)}, u32[]{:S(2)}) collective-permute-start(bf16[256,2,2048]{0,2,1:T(8,128)(2,1)S(1)} %collective-permute-done), channel_id=1, source_target_pairs={{0,1},{1,2},{2,3},{3,4},{4,5},{5,6},{6,7},{7,0},{8,9},{9,10},{10,1... | collective-permute-start | bytes 6291464 | tf_op jit(solution)/shard_map/ppermute | solution.py:23
  478.2 1.4 copy-start.2
  479.5 27.3 %collective-permute-start.2 = (bf16[256,2,2048]{0,2,1:T(8,128)(2,1)S(1)}, bf16[256,2,2048]{0,2,1:T(8,128)(2,1)S(1)}, u32[]{:S(2)}, u32[]{:S(2)}) collective-permute-start(bf16[256,2,2048]{0,2,1:T(8,128)(2,1)S(1)} %collective-permute-done.1), channel_id=1, source_target_pairs={{0,1},{1,2},{2,3},{3,4},{4,5},{5,6},{6,7},{7,0},{8,9},{9,10},{10,1... | collective-permute-start | bytes 6291464 | tf_op jit(solution)/shard_map/ppermute | solution.py:23
  506.8 1.3 copy-start.4
  508.1 27.3 %collective-permute-start.3 = (bf16[256,2,2048]{0,2,1:T(8,128)(2,1)S(1)}, bf16[256,2,2048]{0,2,1:T(8,128)(2,1)S(1)}, u32[]{:S(2)}, u32[]{:S(2)}) collective-permute-start(bf16[256,2,2048]{0,2,1:T(8,128)(2,1)S(1)} %collective-permute-done.2), channel_id=1, source_target_pairs={{0,1},{1,2},{2,3},{3,4},{4,5},{5,6},{6,7},{7,0},{8,9},{9,10},{10,1... | collective-permute-start | bytes 6291464 | tf_op jit(solution)/shard_map/ppermute | solution.py:23
  535.4 1.3 copy-start.6
  536.7 27.3 %collective-permute-start.4 = (bf16[256,2,2048]{0,2,1:T(8,128)(2,1)S(1)}, bf16[256,2,2048]{0,2,1:T(8,128)(2,1)S(1)}, u32[]{:S(2)}, u32[]{:S(2)}) collective-permute-start(bf16[256,2,2048]{0,2,1:T(8,128)(2,1)S(1)} %collective-permute-done.3), channel_id=1, source_target_pairs={{0,1},{1,2},{2,3},{3,4},{4,5},{5,6},{6,7},{7,0},{8,9},{9,10},{10,1... | collective-permute-start | bytes 6291464 | tf_op jit(solution)/shard_map/ppermute | solution.py:23
  563.9 1.3 copy-start.8
  565.3 27.4 %collective-permute-start.5 = (bf16[256,2,2048]{0,2,1:T(8,128)(2,1)S(1)}, bf16[256,2,2048]{0,2,1:T(8,128)(2,1)}, u32[]{:S(2)}, u32[]{:S(2)}) collective-permute-start(bf16[256,2,2048]{0,2,1:T(8,128)(2,1)S(1)} %collective-permute-done.4), channel_id=1, source_target_pairs={{0,1},{1,2},{2,3},{3,4},{4,5},{5,6},{6,7},{7,0},{8,9},{9,10},{10,1... | collective-permute-start | bytes 6291464 | tf_op jit(solution)/shard_map/ppermute | solution.py:23
  592.6 27.6 %collective-permute-start.6 = (bf16[256,2,2048]{0,2,1:T(8,128)(2,1)}, bf16[256,2,2048]{0,2,1:T(8,128)(2,1)}, u32[]{:S(2)}, u32[]{:S(2)}) collective-permute-start(bf16[256,2,2048]{0,2,1:T(8,128)(2,1)} %collective-permute-done.5), channel_id=1, source_target_pairs={{0,1},{1,2},{2,3},{3,4},{4,5},{5,6},{6,7},{7,0},{8,9},{9,10},{10,1... | collective-permute-start | bytes 6291464 | tf_op jit(solution)/shard_map/ppermute | solution.py:23
  614.5 9.6 %copy-start.9 = (bf16[256,2,2048]{0,2,1:T(8,128)(2,1)S(1)}, bf16[256,2,2048]{0,2,1:T(8,128)(2,1)}, u32[]{:S(2)}) copy-start(bf16[256,2,2048]{0,2,1:T(8,128)(2,1)} %copy-done.8) | copy-start | bytes 6291460
  622.1 2.4 copy-start.7
  624.2 1.6 copy-start.5
  624.5 2.0 copy-start.3
  625.8 1.7 copy-start.1
Sparse Core Ops, SparseCore 0:
  33.0 328.1 reduce-scatter.1
